TPU v7x, 32 devices: a whole 2x2x4 slice. The times are simulated.
32 devices in a mesh: dp: 8 (over z, x), tp: 4 (over y, core).
Axes of the slice: x: 2, y: 2, z: 4, core: 2. Of those that a mesh axis runs over, the one named last changes fastest.
Arguments:
- hidden_in: bfloat16 [512, 3584], P(('dp', 'tp')), may hold values from -6 to 6
- query_latent: bfloat16 [512, 64, 512], P(('dp', 'tp')), may hold values from -348 to 347
- query_rope: bfloat16 [512, 4096], P(('dp', 'tp')), may hold values from -348 to 347
- cache_latent: bfloat16 [512, 128, 512], P(('dp', 'tp')), may hold values from -6 to 6
- cache_rope: bfloat16 [512, 64, 128], P(('dp', 'tp')), may hold values from -6 to 6
- lengths: int32 [512], P(('dp', 'tp')), may hold values from 16 to 128
- value_up: bfloat16 [512, 4096], P(None, 'tp'), may hold values from -1 to 1
- out_proj: bfloat16 [4096, 3584], P('tp'), may hold values from -0.09375 to 0.09375
- norm_gain: float32 [3584], replicated, may hold values from 0.1 to 1.9
- expert_gate: bfloat16 [32, 3584, 1024], P(('dp', 'tp')), may hold values from -0.09375 to 0.09375
- expert_down: bfloat16 [32, 1024, 3584], P(('dp', 'tp')), may hold values from -0.1875 to 0.1875
- expert_ids: int32 [512, 8], P(('dp', 'tp')), may hold values from 0 to 31, all different within a row; in each aligned block of 16 rows (0 to 15, 16 to 31, ...) at most 4 rows name the same one
- affinity: float32 [512, 8], P(('dp', 'tp')), may hold values from 0.05 to 1
Outputs:
- layer_out: bfloat16 [512, 3584], P(('dp', 'tp'))
Inputs may be any that keep to these rules, and one draw needn't show every extreme that they name: `expert_ids`: in each aligned block of 16 rows (the rows of one device) no expert is named by more than 4 rows.
All inputs are finite; a program needn't handle non-finite values.
Results may differ from a plain program's by a relative error of at most 0.0081.
Values may be sent and summed in bfloat16 or wider, within the bound.
A program may use at most 128 MiB of HBM per device.

v0:
```python
import jax
import jax.numpy as jnp
from jax import lax
from jax.sharding import PartitionSpec as P

score_scale = 192.0 ** (-0.5)
norm_eps = 1e-06
route_scale = 2.5


def attend(query_latent, query_rope, cache_latent, cache_rope, lengths):
    token_count, head_count, latent_width = query_latent.shape
    rope_width = cache_rope.shape[1]
    context = cache_latent.shape[1]
    query_rot = query_rope.reshape(token_count, head_count, rope_width)
    scores = jnp.einsum(
        "thl,tpl->thp", query_latent, cache_latent, preferred_element_type=jnp.float32
    )
    scores = scores + jnp.einsum(
        "thr,trp->thp", query_rot, cache_rope, preferred_element_type=jnp.float32
    )
    scores = scores * score_scale
    position = lax.broadcasted_iota(jnp.int32, (token_count, 1, context), 2)
    scores = jnp.where(position < lengths[:, None, None], scores, -jnp.inf)
    row_max = jnp.max(scores, axis=2, keepdims=True)
    raised = jnp.exp(scores - row_max)
    attn_weights = (raised / jnp.sum(raised, axis=2, keepdims=True)).astype(jnp.bfloat16)
    latent_out = jnp.einsum(
        "thp,tpl->thl", attn_weights, cache_latent, preferred_element_type=jnp.float32
    )
    return latent_out.astype(jnp.bfloat16)


def per_device(
    hidden_in,
    query_latent,
    query_rope,
    cache_latent,
    cache_rope,
    lengths,
    value_up,
    out_proj,
    norm_gain,
    expert_gate,
    expert_down,
    expert_ids,
    affinity,
):
    latent_out = attend(query_latent, query_rope, cache_latent, cache_rope, lengths)
    group_size = lax.axis_size("tp")
    local_heads = latent_out.shape[1] // group_size
    by_heads = lax.all_to_all(latent_out, "tp", split_axis=1, concat_axis=0, tiled=True)
    head_width = value_up.shape[1] // local_heads
    up_table = value_up.reshape(value_up.shape[0], local_heads, head_width)
    per_head = jnp.einsum(
        "thl,lhv->thv", by_heads, up_table, preferred_element_type=jnp.float32
    ).astype(jnp.bfloat16)
    attn_sum = lax.psum_scatter(
        jnp.dot(
            per_head.reshape(hidden_in.shape[0] * lax.axis_size("tp"), local_heads * head_width),
            out_proj,
            preferred_element_type=jnp.float32,
        ),
        "tp",
        scatter_dimension=0,
        tiled=True,
    )
    hidden = (hidden_in.astype(jnp.float32) + attn_sum).astype(jnp.bfloat16)
    wide_hidden = hidden.astype(jnp.float32)
    inv_norm = lax.rsqrt(jnp.mean(wide_hidden * wide_hidden, axis=1, keepdims=True) + norm_eps)
    normed = (wide_hidden * inv_norm * norm_gain).astype(jnp.bfloat16)
    tok_rows, top_count = expert_ids.shape
    width = normed.shape[1]
    experts = expert_gate.shape[0] * lax.axis_size("dp") * lax.axis_size("tp")
    capacity = max(2, -(-(tok_rows * top_count) // experts))
    flat_ids = expert_ids.reshape(-1)
    expert_iota = lax.broadcasted_iota(jnp.int32, (1, experts), 1)
    one_hot = (flat_ids[:, None] == expert_iota).astype(jnp.int32)
    earlier = jnp.cumsum(one_hot, axis=0) - one_hot
    slot_index = jnp.sum(earlier * one_hot, axis=1)
    target = flat_ids * capacity + slot_index
    owner_row = jnp.arange(tok_rows * top_count, dtype=jnp.int32) // top_count
    source_row = jnp.full((experts * capacity,), tok_rows, jnp.int32).at[target].set(owner_row)
    padded = jnp.concatenate([normed, jnp.zeros((1, width), jnp.bfloat16)], axis=0)
    outgoing = padded[source_row].reshape(experts, capacity, width)
    gate_local = expert_gate[0]
    down_local = expert_down[0]
    slot_rows = lax.all_to_all(outgoing, ("dp", "tp"), split_axis=0, concat_axis=0, tiled=True)
    lead_shape = slot_rows.shape[:-1]
    flat_rows = slot_rows.reshape(-1, width)
    inner_act = jax.nn.silu(
        jnp.dot(flat_rows, gate_local, preferred_element_type=jnp.float32)
    ).astype(jnp.bfloat16)
    answer = jnp.dot(inner_act, down_local, preferred_element_type=jnp.float32).astype(jnp.bfloat16)
    answered = answer.reshape(lead_shape + (width,))
    returned = lax.all_to_all(answered, ("dp", "tp"), split_axis=0, concat_axis=0, tiled=True)
    returned = returned.reshape(experts * capacity, width)
    picked = returned[target].reshape(tok_rows, top_count, width).astype(jnp.float32)
    route_weight = route_scale * affinity / jnp.sum(affinity, axis=1, keepdims=True)
    moe_sum = jnp.sum(picked * route_weight[:, :, None], axis=1)
    return (wide_hidden + moe_sum).astype(jnp.bfloat16)


def solution(mesh):
    return jax.shard_map(
        per_device,
        mesh=mesh,
        in_specs=(
            P(("dp", "tp"), None),
            P(("dp", "tp"), None, None),
            P(("dp", "tp"), None),
            P(("dp", "tp"), None, None),
            P(("dp", "tp"), None, None),
            P(("dp", "tp")),
            P(None, "tp"),
            P("tp", None),
            P(),
            P(("dp", "tp"), None, None),
            P(("dp", "tp"), None, None),
            P(("dp", "tp"), None),
            P(("dp", "tp"), None),
        ),
        out_specs=P(("dp", "tp"), None),
        check_vma=False,
    )
```

profile of v0, /device:TPU:0, one launch (start us, length us, event | category | flops | bytes accessed | tf_op | source)
XLA Modules:
  0.0 151.1 jit_solution(3148003885721317271)
XLA Ops:
  6.5 0.0 copy-start
  6.5 1.3 reshape.85
  7.9 0.7 iota_compare_fusion.1
  8.6 1.2 fusion.31
  9.8 0.0 copy-done
  9.8 2.1 %fusion.12 = f32[16,64,128]{2,1,0:T(8,128)S(1)} fusion(f32[16,64,128]{2,1,0:T(8,128)S(1)} %fusion.31, bf16[16,64,512]{2,1,0:T(8,128)(2,1)} %param.14, bf16[16,128,512]{2,1,0:T(8,128)(2,1)S(1)} %copy-done, pred[16,128]{1,0:T(8,128)(4,1)S(1)} %iota_compare_fusion.1), kind=kOutput, calls=%fused_computation.16 | convolution fusion | flops 134610944 | bytes 4196352 | tf_op jit(solution)/shard_map/thl,tpl->thp/dot_general | solution.py:16
  11.8 0.3 fusion.30
  12.2 3.0 %convolution_convert_fusion = bf16[16,64,512]{2,1,0:T(8,128)(2,1)} fusion(bf16[16,128,512]{2,1,0:T(8,128)(2,1)S(1)} %copy-done, f32[16,64]{1,0:T(8,128)S(1)} %fusion.30, f32[16,64,128]{2,1,0:T(8,128)S(1)} %fusion.12), kind=kOutput, calls=%fused_computation.11 | convolution fusion | flops 135136384 | bytes 3674112 | tf_op jit(solution)/shard_map/thp,tpl->thl/dot_general | solution.py:28
  15.2 2.8 %copy.25 = bf16[16,64,512]{2,0,1:T(8,128)(2,1)} copy(bf16[16,64,512]{2,1,0:T(8,128)(2,1)} %convolution_convert_fusion) | data formatting | bytes 2097152 | tf_op jit(solution)/shard_map/convert_element_type | solution.py:31
  18.0 4.3 %all-to-all-start = ((bf16[16,64,512]{2,0,1:T(8,128)(2,1)}), bf16[16,64,512]{2,0,1:T(8,128)(2,1)S(1)}, u32[]{:S(2)}, u32[]{:S(2)}) async-start(bf16[16,64,512]{2,0,1:T(8,128)(2,1)} %copy.25), calls=%async_computation | async-start | bytes 2097152 | tf_op jit(solution)/shard_map/all_to_all | solution.py:52
  22.2 0.0 reduce-scatter.2.cloned.1.call-start
  22.2 2.3 %copy.27 = bf16[512,1024]{0,1:T(8,128)(2,1)} copy(bf16[512,1024]{1,0:T(8,128)(2,1)} %param.19) | data formatting | bytes 2097152 | tf_op args[6]
  24.5 12.1 %all-to-all-done = bf16[16,64,512]{2,0,1:T(8,128)(2,1)S(1)} async-done(((bf16[16,64,512]{2,0,1:T(8,128)(2,1)}), bf16[16,64,512]{2,0,1:T(8,128)(2,1)S(1)}, u32[]{:S(2)}, u32[]{:S(2)}) %all-to-all-start) | async-done | bytes 1048608 | tf_op jit(solution)/shard_map/all_to_all | solution.py:52
  36.6 0.1 copy.26
  36.7 1.6 %fusion.13 = bf16[64,16,64]{2,0,1:T(8,128)(2,1)S(1)} fusion(bf16[64,16,512]{2,0,1:T(8,128)(2,1)S(1)} %bitcast.42, bf16[512,16,64]{0,2,1:T(8,128)(2,1)} %bitcast.41), kind=kOutput, calls=%fused_computation.18 | convolution fusion | flops 67174400 | bytes 2228224 | tf_op jit(solution)/shard_map/thl,lhv->thv/dot_general | solution.py:55
  38.4 0.2 copy.28
  38.6 0.2 reshape.87
  38.8 0.0 copy-start.2
  38.8 0.0 copy-start.1
  38.8 0.0 copy-start.4
  38.8 5.4 %fusion.32 = f32[64,3584]{1,0:T(8,128)} fusion(bf16[64,1024]{1,0:T(8,128)(2,1)S(1)} %reshape.87, bf16[1024,3584]{1,0:T(8,128)(2,1)} %param.20), kind=kOutput, calls=%fused_computation.54 | convolution fusion | flops 469762048 | bytes 8388608 | tf_op jit(solution)/shard_map/dot_general | solution.py:59
  44.2 0.0 reduce-scatter.2.cloned.1.call-update
  44.3 0.0 copy-done.2
  44.3 0.1 copy.30
  44.3 0.1 eq.15
  44.4 0.1 copy.29
  44.5 0.1 mul.71
  44.6 0.1 fusion.24
  44.7 0.2 reduce_window_sum.11
  44.9 0.2 select_reduce_fusion
  45.1 1.0 scatter_custom_fusion
  46.1 23.4 %reduce-scatter.2.cloned.1.call-done = f32[16,3584]{1,0:T(8,128)} async-done(((f32[64,3584]{1,0:T(8,128)}), f32[16,3584]{1,0:T(8,128)}) %reduce-scatter.2.cloned.1.call-update) | async-done | bytes 229392 | tf_op jit(solution)/shard_map/reduce_scatter | solution.py:58
  69.4 0.0 copy-done.1
  69.4 1.1 fusion.20
  70.5 0.1 fusion.22
  70.7 1.1 gather_fusion
  71.8 1.1 reshape.88
  72.9 28.0 %all_to_all.28 = bf16[32,4,3584]{2,1,0:T(4,128)(2,1)S(1)} all-to-all(bf16[32,4,3584]{2,1,0:T(4,128)(2,1)} %reshape.88), channel_id=1, replica_groups=mesh['dp'=8,'tp'=4] {'dp','tp'}, dimensions={0} | all-to-all | bytes 1835008 | tf_op jit(solution)/shard_map/all_to_all | solution.py:88
  100.9 1.1 reshape.89
  102.1 7.6 %fusion.5 = bf16[128,3584]{1,0:T(8,128)(2,1)S(1)} fusion(bf16[1,1024,3584]{2,1,0:T(8,128)(2,1)} %param.23, bf16[128,3584]{1,0:T(8,128)(2,1)} %reshape.89, bf16[1,3584,1024]{2,1,0:T(8,128)(2,1)} %param.22), kind=kOutput, calls=%fused_computation.8 | convolution fusion | flops 1880162304 | bytes 16515072 | tf_op jit(solution)/shard_map/dot_general | solution.py:94
  109.7 1.2 reshape.90
  110.9 3.7 %all-to-all-start.2 = ((bf16[32,4,3584]{2,1,0:T(4,128)(2,1)}), bf16[32,4,3584]{2,1,0:T(4,128)(2,1)}, u32[]{:S(2)}, u32[]{:S(2)}) async-start(bf16[32,4,3584]{2,1,0:T(4,128)(2,1)} %reshape.90), calls=%async_computation.3 | async-start | bytes 1835008 | tf_op jit(solution)/shard_map/all_to_all | solution.py:96
  114.7 0.1 copy.31
  114.7 23.3 %all-to-all-done.2 = bf16[32,4,3584]{2,1,0:T(4,128)(2,1)} async-done(((bf16[32,4,3584]{2,1,0:T(4,128)(2,1)}), bf16[32,4,3584]{2,1,0:T(4,128)(2,1)}, u32[]{:S(2)}, u32[]{:S(2)}) %all-to-all-start.2) | async-done | bytes 917536 | tf_op jit(solution)/shard_map/all_to_all | solution.py:96
  138.0 1.7 %reshape.91 = bf16[128,3584]{1,0:T(8,128)(2,1)S(1)} reshape(bf16[32,4,3584]{2,1,0:T(4,128)(2,1)} %all-to-all-done.2) | data formatting | bytes 1835008 | tf_op jit(solution)/shard_map/reshape | solution.py:97
  139.7 2.0 %gather_fusion.1 = bf16[128,3584]{1,0:T(8,128)(2,1)} fusion(bf16[128,3584]{1,0:T(8,128)(2,1)S(1)} %reshape.91, s32[1024]{0:T(1024)S(1)} %pad_clamp_fusion), kind=kCustom, calls=%fused_computation.1 | custom fusion | bytes 1835520 | tf_op jit(solution)/shard_map/gather | solution.py:98
  141.7 1.9 %fusion.8 = f32[16,3584]{1,0:T(8,128)S(1)} fusion(bf16[128,3584]{1,0:T(8,128)(2,1)} %gather_fusion.1, f32[16,8]{1,0:T(8,128)S(1)} %copy.31), kind=kLoop, calls=%fused_computation.10 | loop fusion | flops 1318912 | bytes 1147392 | tf_op jit(solution)/shard_map/reduce_sum | solution.py:100
  143.6 0.7 fusion.23
  (13 shorter events, 0.1 us)
Async XLA Ops:
  6.5 3.2 %copy-start = (bf16[16,128,512]{2,1,0:T(8,128)(2,1)S(1)}, bf16[16,128,512]{2,1,0:T(8,128)(2,1)}, u32[]{:S(2)}) copy-start(bf16[16,128,512]{2,1,0:T(8,128)(2,1)} %param.16) | copy-start | bytes 6291460
  18.0 18.7 %all-to-all-start = ((bf16[16,64,512]{2,0,1:T(8,128)(2,1)}), bf16[16,64,512]{2,0,1:T(8,128)(2,1)S(1)}, u32[]{:S(2)}, u32[]{:S(2)}) async-start(bf16[16,64,512]{2,0,1:T(8,128)(2,1)} %copy.25), calls=%async_computation | async-start | bytes 2097152 | tf_op jit(solution)/shard_map/all_to_all | solution.py:52
  22.2 47.2 %reduce-scatter.2.cloned.1.call-start = ((), (), s32[]{:S(2)}) async-start(), calls=%async_computation.4 | async-start | bytes 1146880 | tf_op jit(solution)/shard_map/reduce_scatter | solution.py:58
  38.8 5.5 %copy-start.2 = (s32[16,8]{0,1:T(8,128)S(1)}, s32[16,8]{0,1:T(8,128)}, u32[]{:S(2)}) copy-start(s32[16,8]{0,1:T(8,128)} %param.24) | copy-start | bytes 1540
  38.8 30.7 %copy-start.1 = (bf16[16,3584]{1,0:T(8,128)(2,1)S(1)}, bf16[16,3584]{1,0:T(8,128)(2,1)}, u32[]{:S(2)}) copy-start(bf16[16,3584]{1,0:T(8,128)(2,1)} %param.13) | copy-start | bytes 344068
  38.8 31.7 %copy-start.4 = (f32[3584]{0:T(1024)S(1)}, f32[3584]{0:T(1024)}, u32[]{:S(2)}) copy-start(f32[3584]{0:T(1024)} %param.21) | copy-start | bytes 43012
  102.1 12.6 %copy-start.3 = (f32[16,8]{0,1:T(8,128)S(1)}, f32[16,8]{0,1:T(8,128)}, u32[]{:S(2)}) copy-start(f32[16,8]{0,1:T(8,128)} %param.25) | copy-start | bytes 1540
  110.9 27.1 %all-to-all-start.2 = ((bf16[32,4,3584]{2,1,0:T(4,128)(2,1)}), bf16[32,4,3584]{2,1,0:T(4,128)(2,1)}, u32[]{:S(2)}, u32[]{:S(2)}) async-start(bf16[32,4,3584]{2,1,0:T(4,128)(2,1)} %reshape.90), calls=%async_computation.3 | async-start | bytes 1835008 | tf_op jit(solution)/shard_map/all_to_all | solution.py:96
Sparse Core Ops, SparseCore 0:
  44.4 25.0 reduce-scatter.1
where the time goes:
time: 152 us; the launch traced here: 151 us
  waiting for transfers between devices  58.8 us (39%)
  blocking collectives  28 us (18%)
  matrix products  20.9 us (14%)
  local copies, waits for them, and re-layouts  16.6 us (11%)
  between operations  13.6 us (9%)
  starting transfers between devices  8 us (5%)
  other arithmetic  5.31 us (3%)
    all_to_all x1, blocking collectives, per_device(): lax.all_to_all(outgoing, ('dp', 'tp'), split_axis=0, concat_axis=0, tiled...  28 us
    reduce_scatter x1, waiting for transfers between devices, per_device(): lax.psum_scatter(jnp.dot(per_head.reshape(hidden_in.shape[0] * lax.axis_s...  23.4 us
    all_to_all x1, waiting for transfers between devices, per_device(): lax.all_to_all(answered, ('dp', 'tp'), split_axis=0, concat_axis=0, tiled...  23.3 us
    all_to_all x1, waiting for transfers between devices, per_device(): lax.all_to_all(latent_out, 'tp', split_axis=1, concat_axis=0, tiled=True)  12.1 us
    dot_general x1, matrix products, per_device(): jnp.dot(inner_act, down_local, preferred_element_type=jnp.float32)  7.64 us
    dot_general x1, matrix products, per_device(): jnp.dot(per_head.reshape(hidden_in.shape[0] * lax.axis_size('tp'), local_...  5.43 us
    all_to_all x1, starting transfers between devices, per_device(): lax.all_to_all(latent_out, 'tp', split_axis=1, concat_axis=0, tiled=True)  4.26 us
    all_to_all x1, starting transfers between devices, per_device(): lax.all_to_all(answered, ('dp', 'tp'), split_axis=0, concat_axis=0, tiled...  3.74 us
  transfers between devices with their start and end apart: 3, of which 3 were waited for; matrix products, arithmetic and copies ran while one was open for 3% of the time, Pallas kernels for 0%

commit v1 on v0

--- a/solution.py
+++ b/solution.py
@@ -1,11 +1,74 @@
+import functools
+
 import jax
 import jax.numpy as jnp
 from jax import lax
+from jax.experimental import pallas as pl
+from jax.experimental.pallas import tpu as pltpu
 from jax.sharding import PartitionSpec as P
 
 score_scale = 192.0 ** (-0.5)
 norm_eps = 1e-06
 route_scale = 2.5
+
+
+def coordinates(axes, index):
+    found = {}
+    for name in reversed(axes):
+        size = lax.axis_size(name)
+        found[name] = lax.rem(index, size)
+        index = lax.div(index, size)
+    return found
+
+
+def flat_index(axes):
+    index = jnp.int32(0)
+    for name in axes:
+        index = index * lax.axis_size(name) + lax.axis_index(name)
+    return index
+
+
+def exchange_kernel(axes, count, block_ref, out_ref, send_sem, recv_sem, own_sem):
+    me = flat_index(axes)
+    barrier = pltpu.get_barrier_semaphore()
+    peers = [coordinates(axes, lax.rem(me + step, count)) for step in range(1, count)]
+    for peer in peers:
+        pl.semaphore_signal(barrier, inc=1, device_id=peer, device_id_type=pl.DeviceIdType.MESH)
+    own = pltpu.make_async_copy(block_ref.at[me], out_ref.at[me], own_sem)
+    own.start()
+    pl.semaphore_wait(barrier, count - 1)
+    copies = []
+    for step in range(1, count):
+        copies.append(
+            pltpu.make_async_remote_copy(
+                src_ref=block_ref.at[lax.rem(me + step, count)],
+                dst_ref=out_ref.at[me],
+                send_sem=send_sem.at[step - 1],
+                recv_sem=recv_sem.at[step - 1],
+                device_id=peers[step - 1],
+                device_id_type=pl.DeviceIdType.MESH,
+            )
+        )
+        copies[-1].start()
+    own.wait()
+    for copy in copies:
+        copy.wait()
+
+
+def exchange(blocks, axes, collective_id):
+    count = blocks.shape[0]
+    return pl.pallas_call(
+        functools.partial(exchange_kernel, axes, count),
+        out_shape=jax.ShapeDtypeStruct(blocks.shape, blocks.dtype),
+        in_specs=[pl.BlockSpec(memory_space=pltpu.VMEM)],
+        out_specs=pl.BlockSpec(memory_space=pltpu.VMEM),
+        scratch_shapes=[
+            pltpu.SemaphoreType.DMA((count - 1,)),
+            pltpu.SemaphoreType.DMA((count - 1,)),
+            pltpu.SemaphoreType.DMA,
+        ],
+        compiler_params=pltpu.CompilerParams(collective_id=collective_id, has_side_effects=True),
+    )(blocks)
 
 
 def attend(query_latent, query_rope, cache_latent, cache_rope, lengths):
@@ -49,22 +112,21 @@
     latent_out = attend(query_latent, query_rope, cache_latent, cache_rope, lengths)
     group_size = lax.axis_size("tp")
     local_heads = latent_out.shape[1] // group_size
-    by_heads = lax.all_to_all(latent_out, "tp", split_axis=1, concat_axis=0, tiled=True)
+    tok_rows, head_count, latent_width = latent_out.shape
+    grouped = latent_out.reshape(tok_rows, group_size, local_heads, latent_width).transpose(1, 0, 2, 3)
+    by_heads = exchange(grouped, ("tp",), 0).reshape(-1, local_heads, latent_width)
     head_width = value_up.shape[1] // local_heads
     up_table = value_up.reshape(value_up.shape[0], local_heads, head_width)
     per_head = jnp.einsum(
         "thl,lhv->thv", by_heads, up_table, preferred_element_type=jnp.float32
     ).astype(jnp.bfloat16)
-    attn_sum = lax.psum_scatter(
-        jnp.dot(
-            per_head.reshape(hidden_in.shape[0] * lax.axis_size("tp"), local_heads * head_width),
-            out_proj,
-            preferred_element_type=jnp.float32,
-        ),
-        "tp",
-        scatter_dimension=0,
-        tiled=True,
-    )
+    partial = jnp.dot(
+        per_head.reshape(group_size * tok_rows, local_heads * head_width),
+        out_proj,
+        preferred_element_type=jnp.float32,
+    ).astype(jnp.bfloat16)
+    partials = exchange(partial.reshape(group_size, tok_rows, -1), ("tp",), 1)
+    attn_sum = jnp.sum(partials.astype(jnp.float32), axis=0)
     hidden = (hidden_in.astype(jnp.float32) + attn_sum).astype(jnp.bfloat16)
     wide_hidden = hidden.astype(jnp.float32)
     inv_norm = lax.rsqrt(jnp.mean(wide_hidden * wide_hidden, axis=1, keepdims=True) + norm_eps)
@@ -85,7 +147,7 @@
     outgoing = padded[source_row].reshape(experts, capacity, width)
     gate_local = expert_gate[0]
     down_local = expert_down[0]
-    slot_rows = lax.all_to_all(outgoing, ("dp", "tp"), split_axis=0, concat_axis=0, tiled=True)
+    slot_rows = exchange(outgoing, ("dp", "tp"), 2)
     lead_shape = slot_rows.shape[:-1]
     flat_rows = slot_rows.reshape(-1, width)
     inner_act = jax.nn.silu(
@@ -93,7 +155,7 @@
     ).astype(jnp.bfloat16)
     answer = jnp.dot(inner_act, down_local, preferred_element_type=jnp.float32).astype(jnp.bfloat16)
     answered = answer.reshape(lead_shape + (width,))
-    returned = lax.all_to_all(answered, ("dp", "tp"), split_axis=0, concat_axis=0, tiled=True)
+    returned = exchange(answered, ("dp", "tp"), 3)
     returned = returned.reshape(experts * capacity, width)
     picked = returned[target].reshape(tok_rows, top_count, width).astype(jnp.float32)
     route_weight = route_scale * affinity / jnp.sum(affinity, axis=1, keepdims=True)

time: 152 us -> 127 us (0.84)
  the two profiles are of different devices: /device:TPU:0 before, /device:TPU:15 now
where the time goes in v1:
time: 127 us
  Pallas kernels  81.9 us (64%)
  matrix products  21.8 us (17%)
  local copies, waits for them, and re-layouts  17.3 us (14%)
  other arithmetic  5.49 us (4%)
    pallas_call x4, Pallas kernels, exchange(): pl.pallas_call(functools.partial(exchange_kernel, axes, count), out_shape...  81.9 us
    dot_general x1, matrix products, per_device(): jnp.dot(inner_act, down_local, preferred_element_type=jnp.float32)  8.33 us
    dot_general x1, matrix products, per_device(): jnp.dot(per_head.reshape(group_size * tok_rows, local_heads * head_width)...  5.29 us
    dot_general x1, matrix products, attend(): jnp.einsum('thp,tpl->thl', attn_weights, cache_latent, preferred_element_...  2.96 us

profile of v1, /device:TPU:15, one launch (start us, length us, event | category | flops | bytes accessed | tf_op | source)
XLA Modules:
  0.0 126.7 jit_solution(18013835054011173275)
XLA Ops:
  0.0 0.0 copy-start
  0.0 1.3 %reshape.94 = bf16[16,64,64]{2,1,0:T(8,128)(2,1)S(1)} reshape(bf16[16,4096]{1,0:T(8,128)(2,1)} %param.15) | data formatting | bytes 262144 | tf_op jit(solution)/shard_map/reshape | solution.py:78
  1.3 1.2 fusion.32
  2.5 0.7 iota_compare_fusion.1
  3.2 0.0 copy-done
  3.2 2.1 %fusion.12 = f32[16,64,128]{2,1,0:T(8,128)S(1)} fusion(f32[16,64,128]{2,1,0:T(8,128)S(1)} %fusion.32, bf16[16,64,512]{2,1,0:T(8,128)(2,1)} %param.14, bf16[16,128,512]{2,1,0:T(8,128)(2,1)S(1)} %copy-done, pred[16,128]{1,0:T(8,128)(4,1)S(1)} %iota_compare_fusion.1), kind=kOutput, calls=%fused_computation.17 | convolution fusion | flops 134610944 | bytes 4196352 | tf_op jit(solution)/shard_map/thl,tpl->thp/dot_general | solution.py:79
  5.3 0.3 fusion.31
  5.6 3.0 %convolution_convert_fusion.1 = bf16[16,64,512]{2,1,0:T(8,128)(2,1)} fusion(bf16[16,128,512]{2,1,0:T(8,128)(2,1)S(1)} %copy-done, f32[16,64]{1,0:T(8,128)S(1)} %fusion.31, f32[16,64,128]{2,1,0:T(8,128)S(1)} %fusion.12), kind=kOutput, calls=%fused_computation.12 | convolution fusion | flops 135136384 | bytes 3674112 | tf_op jit(solution)/shard_map/thp,tpl->thl/dot_general | solution.py:91
  8.6 2.3 %copy.29 = bf16[16,4,16,512]{3,2,0,1:T(8,128)(2,1)} copy(bf16[16,4,16,512]{3,2,1,0:T(8,128)(2,1)} %bitcast.43) | data formatting | bytes 2097152 | tf_op jit(solution)/shard_map/reshape | solution.py:116
  10.9 16.5 %shard_map.127 = bf16[4,16,16,512]{3,2,1,0:T(8,128)(2,1)} custom-call(bf16[4,16,16,512]{3,2,1,0:T(8,128)(2,1)} %bitcast.41), custom_call_target="tpu_custom_call" | custom-call | tf_op jit(solution)/shard_map/pallas_call | solution.py:60
  27.5 1.5 %copy.20 = bf16[512,1024]{0,1:T(8,128)(2,1)S(1)} copy(bf16[512,1024]{1,0:T(8,128)(2,1)} %param.19) | data formatting | bytes 2097152 | tf_op args[6]
  29.0 2.0 %fusion.13 = bf16[64,16,64]{2,0,1:T(8,128)(2,1)S(1)} fusion(bf16[512,16,64]{0,2,1:T(8,128)(2,1)S(1)} %bitcast.45, bf16[64,16,512]{2,1,0:T(8,128)(2,1)} %bitcast.44), kind=kOutput, calls=%fused_computation.19 | convolution fusion | flops 67174400 | bytes 2228224 | tf_op jit(solution)/shard_map/thl,lhv->thv/dot_general | solution.py:120
  30.9 0.2 copy.22
  31.1 0.2 reshape.98
  31.3 0.0 copy-start.1
  31.3 0.0 copy-start.4
  31.3 0.0 copy-start.2
  31.4 5.3 %convolution_convert_fusion = bf16[64,3584]{1,0:T(8,128)(2,1)} fusion(bf16[64,1024]{1,0:T(8,128)(2,1)S(1)} %reshape.98, bf16[1024,3584]{1,0:T(8,128)(2,1)} %param.20), kind=kOutput, calls=%fused_computation.9 | convolution fusion | flops 469991424 | bytes 7929856 | tf_op jit(solution)/shard_map/dot_general | solution.py:123
  36.6 9.2 %shard_map.128 = bf16[4,16,3584]{2,1,0:T(8,128)(2,1)} custom-call(bf16[4,16,3584]{2,1,0:T(8,128)(2,1)} %bitcast.42), custom_call_target="tpu_custom_call" | custom-call | tf_op jit(solution)/shard_map/pallas_call | solution.py:60
  45.8 1.1 convert_reduce_fusion
  46.9 0.0 copy-done.1
  47.0 0.2 fusion.21
  47.1 0.0 copy-done.4
  47.1 0.1 fusion.23
  47.3 0.0 copy-done.2
  47.3 0.1 copy.24
  47.3 0.1 eq.15
  47.4 0.1 fusion.25
  47.5 0.2 reduce_window_sum.11
  47.7 0.2 select_reduce_fusion
  47.9 0.1 copy.23
  48.0 0.1 mul.71
  48.1 1.2 scatter_custom_fusion
  49.3 1.1 gather_fusion
  50.4 1.1 reshape.100.block_ref
  51.5 28.2 %shard_map.129 = bf16[32,4,3584]{2,1,0:T(4,128)(2,1)} custom-call(bf16[32,4,3584]{2,1,0:T(4,128)(2,1)} %reshape.100.block_ref), custom_call_target="tpu_custom_call" | custom-call | tf_op jit(solution)/shard_map/pallas_call | solution.py:60
  79.7 1.7 %reshape.101 = bf16[128,3584]{1,0:T(8,128)(2,1)S(1)} reshape(bf16[32,4,3584]{2,1,0:T(4,128)(2,1)} %shard_map.129) | data formatting | bytes 1835008 | tf_op jit(solution)/shard_map/reshape | solution.py:152
  81.4 8.3 %fusion.5 = bf16[128,3584]{1,0:T(8,128)(2,1)} fusion(bf16[1,1024,3584]{2,1,0:T(8,128)(2,1)} %param.23, bf16[128,3584]{1,0:T(8,128)(2,1)S(1)} %reshape.101, bf16[1,3584,1024]{2,1,0:T(8,128)(2,1)} %param.22), kind=kOutput, calls=%fused_computation.8 | convolution fusion | flops 1880162304 | bytes 16515072 | tf_op jit(solution)/shard_map/dot_general | solution.py:156
  89.7 0.0 copy-start.3
  89.7 2.5 %reshape.102.block_ref = bf16[32,4,3584]{2,1,0:T(4,128)(2,1)} reshape(bf16[128,3584]{1,0:T(8,128)(2,1)} %fusion.5) | data formatting | bytes 1835008 | tf_op jit(solution)/shard_map/reshape | solution.py:157
  92.3 28.0 %shard_map.130 = bf16[32,4,3584]{2,1,0:T(4,128)(2,1)} custom-call(bf16[32,4,3584]{2,1,0:T(4,128)(2,1)} %reshape.102.block_ref), custom_call_target="tpu_custom_call" | custom-call | tf_op jit(solution)/shard_map/pallas_call | solution.py:60
  120.3 1.7 %reshape.103 = bf16[128,3584]{1,0:T(8,128)(2,1)S(1)} reshape(bf16[32,4,3584]{2,1,0:T(4,128)(2,1)} %shard_map.130) | data formatting | bytes 1835008 | tf_op jit(solution)/shard_map/reshape | solution.py:159
  122.0 2.1 %gather_fusion.1 = bf16[128,3584]{1,0:T(8,128)(2,1)} fusion(bf16[128,3584]{1,0:T(8,128)(2,1)S(1)} %reshape.103, s32[1024]{0:T(1024)S(1)} %pad_clamp_fusion), kind=kCustom, calls=%fused_computation.1 | custom fusion | bytes 1835520 | tf_op jit(solution)/shard_map/gather | solution.py:160
  124.0 0.0 copy-done.3
  124.0 0.1 copy.25
  124.1 1.9 %fusion.8 = f32[16,3584]{1,0:T(8,128)S(1)} fusion(bf16[128,3584]{1,0:T(8,128)(2,1)} %gather_fusion.1, f32[16,8]{1,0:T(8,128)S(1)} %copy.25), kind=kLoop, calls=%fused_computation.11 | loop fusion | flops 1318912 | bytes 1147392 | tf_op jit(solution)/shard_map/reduce_sum | solution.py:162
  126.0 0.7 fusion.24
  (10 shorter events, 0.1 us)
Async XLA Ops:
  0.0 3.2 %copy-start = (bf16[16,128,512]{2,1,0:T(8,128)(2,1)S(1)}, bf16[16,128,512]{2,1,0:T(8,128)(2,1)}, u32[]{:S(2)}) copy-start(bf16[16,128,512]{2,1,0:T(8,128)(2,1)} %param.16) | copy-start | bytes 6291460
  31.3 15.6 %copy-start.1 = (bf16[16,3584]{1,0:T(8,128)(2,1)S(1)}, bf16[16,3584]{1,0:T(8,128)(2,1)}, u32[]{:S(2)}) copy-start(bf16[16,3584]{1,0:T(8,128)(2,1)} %param.13) | copy-start | bytes 344068
  31.3 15.8 %copy-start.4 = (f32[3584]{0:T(1024)S(1)}, f32[3584]{0:T(1024)}, u32[]{:S(2)}) copy-start(f32[3584]{0:T(1024)} %param.21) | copy-start | bytes 43012
  31.3 15.9 %copy-start.2 = (s32[16,8]{0,1:T(8,128)S(1)}, s32[16,8]{0,1:T(8,128)}, u32[]{:S(2)}) copy-start(s32[16,8]{0,1:T(8,128)} %param.24) | copy-start | bytes 1540
  89.7 34.3 %copy-start.3 = (f32[16,8]{0,1:T(8,128)S(1)}, f32[16,8]{0,1:T(8,128)}, u32[]{:S(2)}) copy-start(f32[16,8]{0,1:T(8,128)} %param.25) | copy-start | bytes 1540

commit v2 on v1

--- a/solution.py
+++ b/solution.py
@@ -131,36 +131,226 @@
     wide_hidden = hidden.astype(jnp.float32)
     inv_norm = lax.rsqrt(jnp.mean(wide_hidden * wide_hidden, axis=1, keepdims=True) + norm_eps)
     normed = (wide_hidden * inv_norm * norm_gain).astype(jnp.bfloat16)
-    tok_rows, top_count = expert_ids.shape
-    width = normed.shape[1]
-    experts = expert_gate.shape[0] * lax.axis_size("dp") * lax.axis_size("tp")
-    capacity = max(2, -(-(tok_rows * top_count) // experts))
-    flat_ids = expert_ids.reshape(-1)
-    expert_iota = lax.broadcasted_iota(jnp.int32, (1, experts), 1)
-    one_hot = (flat_ids[:, None] == expert_iota).astype(jnp.int32)
-    earlier = jnp.cumsum(one_hot, axis=0) - one_hot
-    slot_index = jnp.sum(earlier * one_hot, axis=1)
-    target = flat_ids * capacity + slot_index
-    owner_row = jnp.arange(tok_rows * top_count, dtype=jnp.int32) // top_count
-    source_row = jnp.full((experts * capacity,), tok_rows, jnp.int32).at[target].set(owner_row)
-    padded = jnp.concatenate([normed, jnp.zeros((1, width), jnp.bfloat16)], axis=0)
-    outgoing = padded[source_row].reshape(experts, capacity, width)
-    gate_local = expert_gate[0]
-    down_local = expert_down[0]
-    slot_rows = exchange(outgoing, ("dp", "tp"), 2)
-    lead_shape = slot_rows.shape[:-1]
-    flat_rows = slot_rows.reshape(-1, width)
-    inner_act = jax.nn.silu(
-        jnp.dot(flat_rows, gate_local, preferred_element_type=jnp.float32)
-    ).astype(jnp.bfloat16)
-    answer = jnp.dot(inner_act, down_local, preferred_element_type=jnp.float32).astype(jnp.bfloat16)
-    answered = answer.reshape(lead_shape + (width,))
-    returned = exchange(answered, ("dp", "tp"), 3)
-    returned = returned.reshape(experts * capacity, width)
-    picked = returned[target].reshape(tok_rows, top_count, width).astype(jnp.float32)
-    route_weight = route_scale * affinity / jnp.sum(affinity, axis=1, keepdims=True)
-    moe_sum = jnp.sum(picked * route_weight[:, :, None], axis=1)
-    return (wide_hidden + moe_sum).astype(jnp.bfloat16)
+    dp, tp = lax.axis_size("dp"), lax.axis_size("tp")
+    inner_dp = 2 if dp % 2 == 0 else 1
+    experts = expert_gate.shape[0] * dp * tp
+    capacity = max(2, -(-expert_ids.size // experts))
+    shape = (dp // inner_dp, inner_dp * tp, inner_dp, tp, capacity)
+    route = routing(expert_ids, affinity, shape)
+    return run_experts(normed, hidden, expert_gate, expert_down, route, shape)
+
+
+def experts_kernel(
+    shape, normed_ref, hidden_ref, route_ref, gate_hbm, down_hbm, out_ref,
+    block, route, sending, received, rows, inner, answers, back, partial, parts,
+    gate, down, weight_sem, far_send, far_recv, route_send, route_recv,
+    near_send, near_recv, own_sem, back_send, back_recv, part_send, part_recv,
+):
+    outer, plane, inner_dp, tp, cap = shape
+    toks, width = normed_ref.shape
+    slots = plane * cap
+    at = lax.axis_index("dp")
+    level = lax.div(at, inner_dp)
+    me = lax.rem(at, inner_dp) * tp + lax.axis_index("tp")
+    chunk = 256
+    gate_copy = pltpu.make_async_copy(gate_hbm.at[0], gate, weight_sem.at[0])
+    down_copy = pltpu.make_async_copy(down_hbm.at[0], down, weight_sem.at[1])
+    gate_copy.start()
+    down_copy.start()
+
+    def far(step):
+        return {"dp": lax.rem(level + step, outer) * inner_dp + lax.rem(at, inner_dp), "tp": lax.axis_index("tp")}
+
+    def near(index):
+        return {"dp": level * inner_dp + lax.div(index, tp), "tp": lax.rem(index, tp)}
+
+    def remote(src, dst, send, recv, device):
+        return pltpu.make_async_remote_copy(
+            src_ref=src, dst_ref=dst, send_sem=send, recv_sem=recv,
+            device_id=device, device_id_type=pl.DeviceIdType.MESH,
+        )
+
+    barrier = pltpu.get_barrier_semaphore()
+    for step in range(1, outer):
+        pl.semaphore_signal(barrier, inc=1, device_id=far(step), device_id_type=pl.DeviceIdType.MESH)
+    for step in range(1, plane):
+        pl.semaphore_signal(
+            barrier, inc=1, device_id=near(lax.rem(me + step, plane)), device_id_type=pl.DeviceIdType.MESH
+        )
+    pl.semaphore_wait(barrier, outer + plane - 2)
+
+    started = []
+    far_copies, route_copies = {}, {}
+    for step in range(1, outer):
+        target = lax.rem(level + step, outer)
+        route_copies[step] = remote(
+            route_ref.at[target], route.at[step], route_send.at[step], route_recv.at[step], far(step)
+        )
+        far_copies[step] = remote(normed_ref, block.at[step], far_send.at[step], far_recv.at[step], far(step))
+        route_copies[step].start()
+        far_copies[step].start()
+
+    near_copies, own_copies = {}, {}
+    for step in range(outer):
+        if step:
+            route_copies[step].wait_recv()
+            far_copies[step].wait_recv()
+            pick, tokens = route[step, :slots, :toks], block[step]
+        else:
+            pick, tokens = route_ref[level, :slots, :toks], normed_ref[...]
+        picked = jnp.dot(pick, tokens, preferred_element_type=jnp.float32).astype(jnp.bfloat16)
+        for index in range(plane):
+            sending[step, index] = picked[index * cap:(index + 1) * cap]
+        own_copies[step] = pltpu.make_async_copy(sending.at[step, me], received.at[me, step], own_sem.at[step])
+        own_copies[step].start()
+        for hop in range(1, plane):
+            peer = lax.rem(me + hop, plane)
+            near_copies[step, hop] = remote(
+                sending.at[step, peer], received.at[me, step],
+                near_send.at[step, hop], near_recv.at[step, hop], near(peer),
+            )
+            near_copies[step, hop].start()
+    for step in range(outer):
+        own_copies[step].wait()
+        for hop in range(1, plane):
+            near_copies[step, hop].wait_recv()
+
+    for index in range(plane):
+        for step in range(outer):
+            first = (index * outer + step) * cap
+            rows[first:first + cap, :] = received[index, step]
+    gate_copy.wait()
+
+    @pl.loop(0, inner.shape[1] // chunk)
+    def _(j):
+        columns = pl.ds(pl.multiple_of(j * chunk, chunk), chunk)
+        pre = jnp.dot(rows[...], gate[:, columns], preferred_element_type=jnp.float32)
+        inner[:, columns] = jax.nn.silu(pre).astype(jnp.bfloat16)
+
+    down_copy.wait()
+
+    @pl.loop(0, width // chunk)
+    def _(j):
+        columns = pl.ds(pl.multiple_of(j * chunk, chunk), chunk)
+        answer = jnp.dot(inner[...], down[:, columns], preferred_element_type=jnp.float32).astype(jnp.bfloat16)
+        for index in range(plane):
+            for step in range(outer):
+                first = (index * outer + step) * cap
+                answers[step, index, :, columns] = answer[first:first + cap]
+
+    back_copies, own_back = {}, {}
+    order = list(range(1, outer)) + [0]
+    for step in order:
+        for hop in range(1, plane):
+            peer = lax.rem(me + hop, plane)
+            back_copies[step, hop] = remote(
+                answers.at[step, peer], back.at[step, me],
+                back_send.at[step, hop], back_recv.at[step, hop], near(peer),
+            )
+            back_copies[step, hop].start()
+        own_back[step] = pltpu.make_async_copy(answers.at[step, me], back.at[step, me], own_sem.at[step])
+        own_back[step].start()
+    part_copies = {}
+    total = hidden_ref[...].astype(jnp.float32)
+    for step in order:
+        own_back[step].wait()
+        for hop in range(1, plane):
+            back_copies[step, hop].wait_recv()
+        arrived = jnp.concatenate([back[step, index] for index in range(plane)], axis=0)
+        if step:
+            high, low = route[step, slots:slots + toks, :slots], route[step, slots + toks:, :slots]
+        else:
+            high, low = route_ref[level, slots:slots + toks, :slots], route_ref[level, slots + toks:, :slots]
+        mixed = jnp.dot(high, arrived, preferred_element_type=jnp.float32) + jnp.dot(
+            low, arrived, preferred_element_type=jnp.float32
+        )
+        if step:
+            partial[step] = mixed.astype(jnp.bfloat16)
+            part_copies[step] = remote(
+                partial.at[step], parts.at[step], part_send.at[step], part_recv.at[step], far(outer - step)
+            )
+            part_copies[step].start()
+        else:
+            total = total + mixed
+    for step in range(1, outer):
+        part_copies[step].wait_recv()
+        total = total + parts[step].astype(jnp.float32)
+    out_ref[...] = total.astype(jnp.bfloat16)
+    for step in range(1, outer):
+        route_copies[step].wait_send()
+        far_copies[step].wait_send()
+        part_copies[step].wait_send()
+    for step in range(outer):
+        for hop in range(1, plane):
+            near_copies[step, hop].wait_send()
+            back_copies[step, hop].wait_send()
+
+
+def run_experts(normed, hidden, expert_gate, expert_down, route, shape):
+    outer, plane, _, _, cap = shape
+    toks, width = normed.shape
+    ff = expert_gate.shape[2]
+    count = outer * plane * cap
+    dma = pltpu.SemaphoreType.DMA
+    vmem = pl.BlockSpec(memory_space=pltpu.VMEM)
+    hbm = pl.BlockSpec(memory_space=pl.ANY)
+    low = jnp.bfloat16
+    return pl.pallas_call(
+        functools.partial(experts_kernel, shape),
+        out_shape=jax.ShapeDtypeStruct((toks, width), low),
+        in_specs=[vmem, vmem, vmem, hbm, hbm],
+        out_specs=vmem,
+        scratch_shapes=[
+            pltpu.VMEM((outer, toks, width), low),
+            pltpu.VMEM(route.shape, low),
+            pltpu.VMEM((outer, plane, cap, width), low),
+            pltpu.VMEM((plane, outer, cap, width), low),
+            pltpu.VMEM((count, width), low),
+            pltpu.VMEM((count, ff), low),
+            pltpu.VMEM((outer, plane, cap, width), low),
+            pltpu.VMEM((outer, plane, cap, width), low),
+            pltpu.VMEM((outer, toks, width), low),
+            pltpu.VMEM((outer, toks, width), low),
+            pltpu.VMEM(expert_gate.shape[1:], low),
+            pltpu.VMEM(expert_down.shape[1:], low),
+            dma((2,)), dma((outer,)), dma((outer,)), dma((outer,)), dma((outer,)),
+            dma((outer, plane)), dma((outer, plane)), dma((outer,)),
+            dma((outer, plane)), dma((outer, plane)), dma((outer,)), dma((outer,)),
+        ],
+        compiler_params=pltpu.CompilerParams(
+            collective_id=2, has_side_effects=True, vmem_limit_bytes=60 * 1024 * 1024
+        ),
+    )(normed, hidden, route, expert_gate, expert_down)
+
+
+def routing(expert_ids, affinity, shape):
+    outer, plane, _, _, cap = shape
+    toks = expert_ids.shape[0]
+    experts = outer * plane
+    weight = route_scale * affinity / jnp.sum(affinity, axis=1, keepdims=True)
+    named = expert_ids[:, :, None] == lax.broadcasted_iota(jnp.int32, (1, 1, experts), 2)
+    chosen = jnp.sum(named.astype(jnp.int32), axis=1)
+    weights = jnp.sum(jnp.where(named, weight[:, :, None], 0.0), axis=1)
+    before = lax.broadcasted_iota(jnp.int32, (toks, toks, 1), 1) < lax.broadcasted_iota(
+        jnp.int32, (toks, toks, 1), 0
+    )
+    rank = jnp.sum(jnp.where(before, chosen[None], 0), axis=1)
+    rank = jnp.where(chosen > 0, rank, -1)
+    in_slot = rank[:, :, None] == lax.broadcasted_iota(jnp.int32, (1, 1, cap), 2)
+    in_slot = in_slot.reshape(toks, outer, plane * cap)
+    spread = jnp.repeat(weights, cap, axis=1).reshape(toks, outer, plane * cap)
+    spread = jnp.where(in_slot, spread, 0.0)
+    high = spread.astype(jnp.bfloat16)
+    rest = (spread - high.astype(jnp.float32)).astype(jnp.bfloat16)
+    lanes = 128 * (-(-max(toks, plane * cap) // 128))
+
+    def padded(array):
+        return jnp.pad(array, ((0, 0), (0, 0), (0, lanes - array.shape[2])))
+
+    pick = padded(in_slot.astype(jnp.bfloat16).transpose(1, 2, 0))
+    return jnp.concatenate(
+        [pick, padded(high.transpose(1, 0, 2)), padded(rest.transpose(1, 0, 2))], axis=1
+    )
 
 
 def solution(mesh):

time: 127 us -> 102 us (0.80)
  the two profiles are of different devices: /device:TPU:15 before, /device:TPU:0 now
where the time goes in v2:
time: 102 us
  Pallas kernels  74.1 us (73%)
  matrix products  13.8 us (14%)
  local copies, waits for them, and re-layouts  8.21 us (8%)
  other arithmetic  5.63 us (6%)
    pallas_call x1, Pallas kernels, run_experts(): pl.pallas_call(functools.partial(experts_kernel, shape), out_shape=jax.Sh...  47.9 us
    pallas_call x2, Pallas kernels, exchange(): pl.pallas_call(functools.partial(exchange_kernel, axes, count), out_shape...  26.2 us
    dot_general x1, matrix products, per_device(): jnp.dot(per_head.reshape(group_size * tok_rows, local_heads * head_width)...  5.27 us
    unnamed x13, local copies, waits for them, and re-layouts  3.68 us
    dot_general x1, matrix products, attend(): jnp.einsum('thp,tpl->thl', attn_weights, cache_latent, preferred_element_...  2.96 us
    reshape x1, local copies, waits for them, and re-layouts, per_device(): latent_out.reshape(tok_rows, group_size, local_heads, latent_width)  2.39 us
    dot_general x1, matrix products, per_device(): jnp.einsum('thl,lhv->thv', by_heads, up_table, preferred_element_type=jnp...  2.28 us
    dot_general x1, matrix products, attend(): jnp.einsum('thl,tpl->thp', query_latent, cache_latent, preferred_element_...  2.07 us

profile of v2, /device:TPU:0, one launch (start us, length us, event | category | flops | bytes accessed | tf_op | source)
XLA Modules:
  0.0 101.9 jit_solution(7413685220086506454)
XLA Ops:
  0.0 0.0 copy-start
  0.0 0.9 reduce_sum.68
  0.9 0.7 iota_compare_fusion.5
  1.6 0.7 multiply_divide_fusion
  2.3 0.1 copy.47
  2.4 0.1 eq.39
  2.4 0.8 copy.44
  3.2 0.1 select_reduce_fusion.1
  3.3 0.1 convert_reduce_fusion.1
  3.4 0.1 select_reduce_fusion
  3.6 0.1 copy.45
  3.6 0.1 copy.48
  3.7 0.1 copy.49
  3.8 0.1 copy.46
  4.0 0.1 copy.50
  4.1 0.6 fusion.15.route_ref
  4.7 1.2 %reshape.69 = bf16[16,64,64]{2,1,0:T(8,128)(2,1)S(1)} reshape(bf16[16,4096]{1,0:T(8,128)(2,1)} %param.15) | data formatting | bytes 262144 | tf_op jit(solution)/shard_map/reshape | solution.py:78
  5.9 1.2 %fusion.20 = f32[16,64,128]{2,1,0:T(8,128)S(1)} fusion(bf16[16,64,64]{2,1,0:T(8,128)(2,1)S(1)} %reshape.69, bf16[16,64,128]{2,1,0:T(8,128)(2,1)} %param.17), kind=kOutput, calls=%fused_computation.46 | convolution fusion | flops 16777216 | bytes 917504 | tf_op jit(solution)/shard_map/thr,trp->thp/dot_general | solution.py:82
  7.0 0.0 copy-done
  7.1 2.1 %fusion.4 = f32[16,64,128]{2,1,0:T(8,128)S(1)} fusion(f32[16,64,128]{2,1,0:T(8,128)S(1)} %fusion.20, bf16[16,64,512]{2,1,0:T(8,128)(2,1)} %param.14, bf16[16,128,512]{2,1,0:T(8,128)(2,1)S(1)} %copy-done, pred[16,128]{1,0:T(8,128)(4,1)S(1)} %iota_compare_fusion.5), kind=kOutput, calls=%fused_computation.7 | convolution fusion | flops 134610944 | bytes 4196352 | tf_op jit(solution)/shard_map/thl,tpl->thp/dot_general | solution.py:79
  9.1 0.3 fusion.19
  9.5 3.0 %convolution_convert_fusion.1 = bf16[16,64,512]{2,1,0:T(8,128)(2,1)} fusion(bf16[16,128,512]{2,1,0:T(8,128)(2,1)S(1)} %copy-done, f32[16,64]{1,0:T(8,128)S(1)} %fusion.19, f32[16,64,128]{2,1,0:T(8,128)S(1)} %fusion.4), kind=kOutput, calls=%fused_computation.2 | convolution fusion | flops 135136384 | bytes 3674112 | tf_op jit(solution)/shard_map/thp,tpl->thl/dot_general | solution.py:91
  12.4 0.0 copy-start.1
  12.4 2.4 %copy.54 = bf16[16,4,16,512]{3,2,0,1:T(8,128)(2,1)} copy(bf16[16,4,16,512]{3,2,1,0:T(8,128)(2,1)} %bitcast.28) | data formatting | bytes 2097152 | tf_op jit(solution)/shard_map/reshape | solution.py:116
  14.8 17.1 %shard_map.127 = bf16[4,16,16,512]{3,2,1,0:T(8,128)(2,1)} custom-call(bf16[4,16,16,512]{3,2,1,0:T(8,128)(2,1)} %bitcast.26), custom_call_target="tpu_custom_call" | custom-call | tf_op jit(solution)/shard_map/pallas_call | solution.py:60
  31.9 0.0 copy-done.1
  31.9 1.3 %copy.41 = bf16[512,1024]{0,1:T(8,128)(2,1)} copy(bf16[512,1024]{1,0:T(8,128)(2,1)S(1)} %copy-done.1) | data formatting | bytes 2097152 | tf_op args[6]
  33.3 2.3 %fusion.5 = bf16[64,16,64]{2,0,1:T(8,128)(2,1)S(1)} fusion(bf16[512,16,64]{0,2,1:T(8,128)(2,1)} %bitcast.30, bf16[64,16,512]{2,1,0:T(8,128)(2,1)} %bitcast.29), kind=kOutput, calls=%fused_computation.9 | convolution fusion | flops 67174400 | bytes 2228224 | tf_op jit(solution)/shard_map/thl,lhv->thv/dot_general | solution.py:120
  35.5 0.2 copy.43
  35.7 0.2 reshape.73
  35.9 0.0 copy-start.3
  35.9 0.0 copy-start.4
  35.9 5.3 %convolution_convert_fusion = bf16[64,3584]{1,0:T(8,128)(2,1)} fusion(bf16[64,1024]{1,0:T(8,128)(2,1)S(1)} %reshape.73, bf16[1024,3584]{1,0:T(8,128)(2,1)} %param.20), kind=kOutput, calls=%fused_computation.1 | convolution fusion | flops 469991424 | bytes 7929856 | tf_op jit(solution)/shard_map/dot_general | solution.py:123
  41.2 9.2 %shard_map.128 = bf16[4,16,3584]{2,1,0:T(8,128)(2,1)} custom-call(bf16[4,16,3584]{2,1,0:T(8,128)(2,1)} %bitcast.27), custom_call_target="tpu_custom_call" | custom-call | tf_op jit(solution)/shard_map/pallas_call | solution.py:60
  50.4 1.1 %convert_reduce_fusion = f32[16,3584]{1,0:T(8,128)S(1)} fusion(bf16[4,16,3584]{2,1,0:T(8,128)(2,1)} %shard_map.128), kind=kLoop, calls=%fused_computation.12 | loop fusion | flops 401408 | bytes 688128 | tf_op jit(solution)/shard_map/reduce_sum | solution.py:129
  51.5 0.0 copy-done.3
  51.5 0.2 fusion.8
  51.7 0.0 copy-start.2
  51.7 0.0 copy-done.4
  51.7 0.7 fusion.10.normed_ref
  52.5 0.0 copy-done.2
  52.5 47.9 %shard_map.129 = bf16[16,3584]{1,0:T(8,128)(2,1)} custom-call(bf16[16,3584]{1,0:T(8,128)(2,1)} %fusion.10.normed_ref, bf16[16,3584]{1,0:T(8,128)(2,1)} %copy-done.2, bf16[4,64,128]{2,1,0:T(8,128)(2,1)} %fusion.15.route_ref, bf16[1,3584,1024]{2,1,0:T(8,128)(2,1)} %gate_hbm.1, bf16[1,1024,3584]{2,1,0:T(8,128)(2,1)} %down_hbm.1), custom_call_target="tpu_custom_call" | custom-call | tf_op jit(solution)/shard_map/pallas_call | solution.py:298
  100.4 1.6 %copy.56 = bf16[16,3584]{1,0:T(8,128)(2,1)} copy(bf16[16,3584]{1,0:T(8,128)(2,1)} %shard_map.129) | data formatting | bytes 229376
  (9 shorter events, 0.1 us)
Async XLA Ops:
  0.0 7.0 %copy-start = (bf16[16,128,512]{2,1,0:T(8,128)(2,1)S(1)}, bf16[16,128,512]{2,1,0:T(8,128)(2,1)}, u32[]{:S(2)}) copy-start(bf16[16,128,512]{2,1,0:T(8,128)(2,1)} %param.16) | copy-start | bytes 6291460
  12.4 19.5 %copy-start.1 = (bf16[512,1024]{1,0:T(8,128)(2,1)S(1)}, bf16[512,1024]{1,0:T(8,128)(2,1)}, u32[]{:S(2)}) copy-start(bf16[512,1024]{1,0:T(8,128)(2,1)} %param.19) | copy-start | bytes 3145732
  35.9 15.6 %copy-start.3 = (bf16[16,3584]{1,0:T(8,128)(2,1)S(1)}, bf16[16,3584]{1,0:T(8,128)(2,1)}, u32[]{:S(2)}) copy-start(bf16[16,3584]{1,0:T(8,128)(2,1)} %param.13) | copy-start | bytes 344068
  35.9 15.8 %copy-start.4 = (f32[3584]{0:T(1024)S(1)}, f32[3584]{0:T(1024)}, u32[]{:S(2)}) copy-start(f32[3584]{0:T(1024)} %param.21) | copy-start | bytes 43012
  51.7 0.8 copy-start.2

commit v3 on v2

--- a/solution.py
+++ b/solution.py
@@ -12,86 +12,163 @@
 route_scale = 2.5
 
 
-def coordinates(axes, index):
-    found = {}
-    for name in reversed(axes):
-        size = lax.axis_size(name)
-        found[name] = lax.rem(index, size)
-        index = lax.div(index, size)
-    return found
-
-
-def flat_index(axes):
-    index = jnp.int32(0)
-    for name in axes:
-        index = index * lax.axis_size(name) + lax.axis_index(name)
-    return index
-
-
-def exchange_kernel(axes, count, block_ref, out_ref, send_sem, recv_sem, own_sem):
-    me = flat_index(axes)
+def attention_kernel(
+    batch, tile, query_hbm, rot_ref, cache_hbm, rope_hbm, lengths_ref, hidden_in_hbm, gain_ref,
+    up_hbm, proj_hbm, hidden_ref, normed_ref, leaving, arrived, heads, partial, parts, total, up, proj,
+    query_ref, cache_ref, rope_ref, hidden_in_ref, weight_sem, input_sem, out_send, out_recv, part_send, part_recv,
+):
+    toks, head_count, latent = query_hbm.shape
+    context = cache_ref.shape[1]
+    group = leaving.shape[0]
+    local = head_count // group
+    width = proj.shape[1]
+    me = lax.axis_index("tp")
+    input_copies = []
+    for number in range(toks // batch):
+        span = pl.ds(number * batch, batch)
+        pairs = ((query_hbm, query_ref), (cache_hbm, cache_ref), (rope_hbm, rope_ref))
+        input_copies.append([
+            pltpu.make_async_copy(src.at[span], dst.at[span], input_sem.at[number, index])
+            for index, (src, dst) in enumerate(pairs)
+        ])
+        for copy in input_copies[-1]:
+            copy.start()
+    hidden_copy = pltpu.make_async_copy(hidden_in_hbm, hidden_in_ref, weight_sem.at[2])
+    up_copy = pltpu.make_async_copy(up_hbm, up, weight_sem.at[0])
+    proj_copy = pltpu.make_async_copy(proj_hbm, proj, weight_sem.at[1])
+    up_copy.start()
+    proj_copy.start()
+    hidden_copy.start()
+    peers = [lax.rem(me + step, group) for step in range(group)]
     barrier = pltpu.get_barrier_semaphore()
-    peers = [coordinates(axes, lax.rem(me + step, count)) for step in range(1, count)]
-    for peer in peers:
-        pl.semaphore_signal(barrier, inc=1, device_id=peer, device_id_type=pl.DeviceIdType.MESH)
-    own = pltpu.make_async_copy(block_ref.at[me], out_ref.at[me], own_sem)
-    own.start()
-    pl.semaphore_wait(barrier, count - 1)
-    copies = []
-    for step in range(1, count):
-        copies.append(
-            pltpu.make_async_remote_copy(
-                src_ref=block_ref.at[lax.rem(me + step, count)],
-                dst_ref=out_ref.at[me],
-                send_sem=send_sem.at[step - 1],
-                recv_sem=recv_sem.at[step - 1],
-                device_id=peers[step - 1],
-                device_id_type=pl.DeviceIdType.MESH,
-            )
-        )
-        copies[-1].start()
-    own.wait()
-    for copy in copies:
-        copy.wait()
-
-
-def exchange(blocks, axes, collective_id):
-    count = blocks.shape[0]
+    for step in range(1, group):
+        pl.semaphore_signal(
+            barrier, inc=1, device_id={"tp": peers[step]}, device_id_type=pl.DeviceIdType.MESH
+        )
+
+    def remote(src, dst, send, recv, step):
+        return pltpu.make_async_remote_copy(
+            src_ref=src, dst_ref=dst, send_sem=send, recv_sem=recv,
+            device_id={"tp": peers[step]}, device_id_type=pl.DeviceIdType.MESH,
+        )
+
+    position = lax.broadcasted_iota(jnp.int32, (head_count, context), 1)
+    out_copies = {}
+    for first in range(0, toks, batch):
+        for copy in input_copies[first // batch]:
+            copy.wait()
+        scores = []
+        for t in range(first, first + batch):
+            score = lax.dot_general(
+                query_ref[t], cache_ref[t], (((1,), (1,)), ((), ())), preferred_element_type=jnp.float32
+            )
+            score = score + jnp.dot(rot_ref[t], rope_ref[t], preferred_element_type=jnp.float32)
+            scores.append(jnp.where(position < lengths_ref[t], score * score_scale, -jnp.inf))
+        weights = []
+        for score in scores:
+            raised = jnp.exp(score - jnp.max(score, axis=1, keepdims=True))
+            weights.append((raised / jnp.sum(raised, axis=1, keepdims=True)).astype(jnp.bfloat16))
+        for offset, weight in enumerate(weights):
+            t = first + offset
+            mixed = jnp.dot(weight, cache_ref[t], preferred_element_type=jnp.float32).astype(jnp.bfloat16)
+            for part in range(group):
+                leaving[part, t] = mixed[part * local:(part + 1) * local]
+        if first == 0:
+            pl.semaphore_wait(barrier, group - 1)
+        span = pl.ds(first, batch)
+        for step in range(1, group):
+            number = first // batch
+            out_copies[number, step] = remote(
+                leaving.at[peers[step], span], arrived.at[step, span],
+                out_send.at[number, step], out_recv.at[number, step], step,
+            )
+            out_copies[number, step].start()
+
+    up_copy.wait()
+    head_width = up.shape[1] // local
+    lane = lax.broadcasted_iota(jnp.int32, (local, up.shape[1]), 1)
+    row = lax.broadcasted_iota(jnp.int32, (local, up.shape[1]), 0)
+    own_head = lax.div(lane, head_width) == row
+    for step in range(group):
+        for first in range(0, toks, batch):
+            if step:
+                out_copies[first // batch, step].wait_recv()
+        source = leaving[me] if step == 0 else arrived[step]
+        flat = source.reshape(toks * local, latent)
+        for column in range(0, up.shape[1], 256):
+            wide = jnp.dot(flat, up[:, column:column + 256], preferred_element_type=jnp.float32)
+            wide = wide.reshape(toks, local, 256)
+            kept = jnp.where(own_head[None, :, column:column + 256], wide, 0.0)
+            heads[step * toks:(step + 1) * toks, column:column + 256] = jnp.sum(kept, axis=1).astype(jnp.bfloat16)
+    proj_copy.wait()
+    part_copies = {}
+    for number in range(width // tile):
+        columns = slice(number * tile, (number + 1) * tile)
+        product = jnp.dot(heads[...], proj[:, columns], preferred_element_type=jnp.float32)
+        total[:, columns] = product[:toks]
+        for step in range(1, group):
+            partial[number, step] = product[step * toks:(step + 1) * toks].astype(jnp.bfloat16)
+            back = group - step
+            part_copies[number, step] = remote(
+                partial.at[number, step], parts.at[number, step],
+                part_send.at[number, step], part_recv.at[number, step], back,
+            )
+            part_copies[number, step].start()
+    hidden_copy.wait()
+    squares = jnp.zeros((toks, 1), jnp.float32)
+    for number in range(width // tile):
+        columns = slice(number * tile, (number + 1) * tile)
+        value = total[:, columns]
+        for step in range(1, group):
+            part_copies[number, step].wait_recv()
+            value = value + parts[number, step].astype(jnp.float32)
+        low = (hidden_in_ref[:, columns].astype(jnp.float32) + value).astype(jnp.bfloat16)
+        hidden_ref[:, columns] = low
+        squares = squares + jnp.sum(low.astype(jnp.float32) * low.astype(jnp.float32), axis=1, keepdims=True)
+    inv_norm = lax.rsqrt(squares / width + norm_eps)
+    normed_ref[...] = (hidden_ref[...].astype(jnp.float32) * inv_norm * gain_ref[...]).astype(jnp.bfloat16)
+    for copy in list(out_copies.values()) + list(part_copies.values()):
+        copy.wait_send()
+
+
+def run_attention(query, rot, cache, rope, lengths, hidden_in, gain, value_up, out_proj):
+    toks, head_count, latent = query.shape
+    group = lax.axis_size("tp")
+    local = head_count // group
+    width = out_proj.shape[1]
+    batch = 4 if toks % 4 == 0 else 1
+    tile = 512 if width % 512 == 0 else 128
+    tiles = width // tile
+    dma = pltpu.SemaphoreType.DMA
+    vmem = pl.BlockSpec(memory_space=pltpu.VMEM)
+    hbm = pl.BlockSpec(memory_space=pl.ANY)
+    smem = pl.BlockSpec(memory_space=pltpu.SMEM)
+    low = jnp.bfloat16
     return pl.pallas_call(
-        functools.partial(exchange_kernel, axes, count),
-        out_shape=jax.ShapeDtypeStruct(blocks.shape, blocks.dtype),
-        in_specs=[pl.BlockSpec(memory_space=pltpu.VMEM)],
-        out_specs=pl.BlockSpec(memory_space=pltpu.VMEM),
+        functools.partial(attention_kernel, batch, tile),
+        out_shape=[jax.ShapeDtypeStruct((toks, width), low)] * 2,
+        in_specs=[hbm, vmem, hbm, hbm, smem, hbm, vmem, hbm, hbm],
+        out_specs=[vmem, vmem],
         scratch_shapes=[
-            pltpu.SemaphoreType.DMA((count - 1,)),
-            pltpu.SemaphoreType.DMA((count - 1,)),
-            pltpu.SemaphoreType.DMA,
+            pltpu.VMEM((group, toks, local, latent), low),
+            pltpu.VMEM((group, toks, local, latent), low),
+            pltpu.VMEM((group * toks, out_proj.shape[0]), low),
+            pltpu.VMEM((tiles, group, toks, tile), low),
+            pltpu.VMEM((tiles, group, toks, tile), low),
+            pltpu.VMEM((toks, width), jnp.float32),
+            pltpu.VMEM(value_up.shape, low),
+            pltpu.VMEM(out_proj.shape, low),
+            pltpu.VMEM(query.shape, low),
+            pltpu.VMEM(cache.shape, low),
+            pltpu.VMEM(rope.shape, low),
+            pltpu.VMEM(hidden_in.shape, low),
+            dma((3,)), dma((toks // batch, 3)), dma((toks // batch, group)), dma((toks // batch, group)),
+            dma((tiles, group)), dma((tiles, group)),
         ],
-        compiler_params=pltpu.CompilerParams(collective_id=collective_id, has_side_effects=True),
-    )(blocks)
-
-
-def attend(query_latent, query_rope, cache_latent, cache_rope, lengths):
-    token_count, head_count, latent_width = query_latent.shape
-    rope_width = cache_rope.shape[1]
-    context = cache_latent.shape[1]
-    query_rot = query_rope.reshape(token_count, head_count, rope_width)
-    scores = jnp.einsum(
-        "thl,tpl->thp", query_latent, cache_latent, preferred_element_type=jnp.float32
-    )
-    scores = scores + jnp.einsum(
-        "thr,trp->thp", query_rot, cache_rope, preferred_element_type=jnp.float32
-    )
-    scores = scores * score_scale
-    position = lax.broadcasted_iota(jnp.int32, (token_count, 1, context), 2)
-    scores = jnp.where(position < lengths[:, None, None], scores, -jnp.inf)
-    row_max = jnp.max(scores, axis=2, keepdims=True)
-    raised = jnp.exp(scores - row_max)
-    attn_weights = (raised / jnp.sum(raised, axis=2, keepdims=True)).astype(jnp.bfloat16)
-    latent_out = jnp.einsum(
-        "thp,tpl->thl", attn_weights, cache_latent, preferred_element_type=jnp.float32
-    )
-    return latent_out.astype(jnp.bfloat16)
+        compiler_params=pltpu.CompilerParams(
+            collective_id=0, has_side_effects=True, vmem_limit_bytes=60 * 1024 * 1024
+        ),
+    )(query, rot, cache, rope, lengths, hidden_in, gain, value_up, out_proj)
 
 
 def per_device(
@@ -109,28 +186,11 @@
     expert_ids,
     affinity,
 ):
-    latent_out = attend(query_latent, query_rope, cache_latent, cache_rope, lengths)
-    group_size = lax.axis_size("tp")
-    local_heads = latent_out.shape[1] // group_size
-    tok_rows, head_count, latent_width = latent_out.shape
-    grouped = latent_out.reshape(tok_rows, group_size, local_heads, latent_width).transpose(1, 0, 2, 3)
-    by_heads = exchange(grouped, ("tp",), 0).reshape(-1, local_heads, latent_width)
-    head_width = value_up.shape[1] // local_heads
-    up_table = value_up.reshape(value_up.shape[0], local_heads, head_width)
-    per_head = jnp.einsum(
-        "thl,lhv->thv", by_heads, up_table, preferred_element_type=jnp.float32
-    ).astype(jnp.bfloat16)
-    partial = jnp.dot(
-        per_head.reshape(group_size * tok_rows, local_heads * head_width),
-        out_proj,
-        preferred_element_type=jnp.float32,
-    ).astype(jnp.bfloat16)
-    partials = exchange(partial.reshape(group_size, tok_rows, -1), ("tp",), 1)
-    attn_sum = jnp.sum(partials.astype(jnp.float32), axis=0)
-    hidden = (hidden_in.astype(jnp.float32) + attn_sum).astype(jnp.bfloat16)
-    wide_hidden = hidden.astype(jnp.float32)
-    inv_norm = lax.rsqrt(jnp.mean(wide_hidden * wide_hidden, axis=1, keepdims=True) + norm_eps)
-    normed = (wide_hidden * inv_norm * norm_gain).astype(jnp.bfloat16)
+    toks, head_count, _ = query_latent.shape
+    hidden, normed = run_attention(
+        query_latent, query_rope.reshape(toks, head_count, -1), cache_latent, cache_rope, lengths,
+        hidden_in, norm_gain.reshape(1, -1), value_up, out_proj,
+    )
     dp, tp = lax.axis_size("dp"), lax.axis_size("tp")
     inner_dp = 2 if dp % 2 == 0 else 1
     experts = expert_gate.shape[0] * dp * tp
@@ -275,7 +335,7 @@
     for step in range(1, outer):
         part_copies[step].wait_recv()
         total = total + parts[step].astype(jnp.float32)
-    out_ref[...] = total.astype(jnp.bfloat16)
+    out_ref[...] = total
     for step in range(1, outer):
         route_copies[step].wait_send()
         far_copies[step].wait_send()
@@ -297,7 +357,7 @@
     low = jnp.bfloat16
     return pl.pallas_call(
         functools.partial(experts_kernel, shape),
-        out_shape=jax.ShapeDtypeStruct((toks, width), low),
+        out_shape=jax.ShapeDtypeStruct((toks, width), jnp.float32),
         in_specs=[vmem, vmem, vmem, hbm, hbm],
         out_specs=vmem,
         scratch_shapes=[
@@ -320,7 +380,7 @@
         compiler_params=pltpu.CompilerParams(
             collective_id=2, has_side_effects=True, vmem_limit_bytes=60 * 1024 * 1024
         ),
-    )(normed, hidden, route, expert_gate, expert_down)
+    )(normed, hidden, route, expert_gate, expert_down).astype(low)
 
 
 def routing(expert_ids, affinity, shape):

time: 102 us -> 79.9 us (0.78)
  matrix products: 13.8 us -> 0 us
  local copies, waits for them, and re-layouts: 8.21 us -> 3.89 us
  other arithmetic: 5.63 us -> 2.65 us
  Pallas kernels: 74.1 us -> 72.7 us
    dot_general x5 -> x0, matrix products: 13.8 us -> none  [the longest x1 5.27 us: per_device(): jnp.dot(per_head.reshape(group_size * tok_rows, local_heads * head_width)...]
    unnamed x13 -> x5, local copies, waits for them, and re-layouts: 3.68 us -> 0.08 us
    pallas_call x1, Pallas kernels: 47.9 us -> 46.3 us  [run_experts(): pl.pallas_call(functools.partial(experts_kernel, shape), out_shape=jax.Sh...]
    reduce_sum x2 -> x0, other arithmetic: 1.26 us -> none  [the longest x1 1.1 us: per_device(): attn_sum = jnp.sum(partials.astype(jnp.float32), axis=0)]
    reshape x3 -> x2, local copies, waits for them, and re-layouts: 3.77 us -> 3.24 us  [the longest x1 1.91 us: per_device(): query_rope.reshape(toks, head_count, -1)]
    pallas_call x2 -> x1, Pallas kernels: 26.2 us -> 26.4 us  [run_attention(): pl.pallas_call(functools.partial(attention_kernel, batch, tile), out_shap...]
where the time goes in v3:
time: 79.9 us; the launch traced here: 79.3 us
  Pallas kernels  72.7 us (91%)
  local copies, waits for them, and re-layouts  3.89 us (5%)
  other arithmetic  2.65 us (3%)
    pallas_call x1, Pallas kernels, run_experts(): pl.pallas_call(functools.partial(experts_kernel, shape), out_shape=jax.Sh...  46.3 us
    pallas_call x1, Pallas kernels, run_attention(): pl.pallas_call(functools.partial(attention_kernel, batch, tile), out_shap...  26.4 us
    reshape x1, local copies, waits for them, and re-layouts, per_device(): query_rope.reshape(toks, head_count, -1)  1.91 us

profile of v3, /device:TPU:0, one launch (start us, length us, event | category | flops | bytes accessed | tf_op | source)
XLA Modules:
  0.0 79.3 jit_solution(15406731281226934017)
XLA Ops:
  0.0 0.0 copy-start
  0.0 0.0 copy-start.1
  0.0 1.9 %reshape.28.rot_ref = bf16[16,64,64]{2,1,0:T(8,128)(2,1)} reshape(bf16[16,4096]{1,0:T(8,128)(2,1)} %param.15) | data formatting | bytes 262144 | tf_op jit(solution)/shard_map/reshape | solution.py:191
  1.9 1.3 %reshape.29.gain_ref = f32[1,3584]{1,0:T(1,128)} reshape(f32[3584]{0:T(1024)} %param.21) | data formatting | bytes 28672 | tf_op jit(solution)/shard_map/reshape | solution.py:192
  3.2 26.4 %shard_map.127 = (bf16[16,3584]{1,0:T(8,128)(2,1)}, bf16[16,3584]{1,0:T(8,128)(2,1)}) custom-call(bf16[16,64,512]{2,1,0:T(8,128)(2,1)} %query_hbm.1, bf16[16,64,64]{2,1,0:T(8,128)(2,1)} %reshape.28.rot_ref, bf16[16,128,512]{2,1,0:T(8,128)(2,1)} %cache_hbm.1, bf16[16,64,128]{2,1,0:T(8,128)(2,1)} %rope_hbm.1, s32[16]{0:T(128)} %lengths_ref.1, ...), custom_call_target="tpu_custom_call" | custom-call | tf_op jit(solution)/shard_map/pallas_call | solution.py:147
  29.6 0.0 copy-done
  29.6 0.1 copy.33
  29.7 0.0 copy-done.1
  29.7 0.1 copy.30
  29.8 0.1 select_reduce_fusion.1
  29.9 0.1 copy.34
  30.0 0.1 copy.35
  30.1 0.1 convert_reduce_fusion
  30.2 0.1 select_reduce_fusion
  30.3 0.1 copy.31
  30.4 0.1 copy.32
  30.5 0.1 eq.39
  30.7 0.1 copy.36
  30.8 0.6 fusion.4.route_ref
  31.4 46.3 %shard_map.128 = f32[16,3584]{1,0:T(8,128)} custom-call(bf16[16,3584]{1,0:T(8,128)(2,1)} %get-tuple-element.7.normed_ref, bf16[16,3584]{1,0:T(8,128)(2,1)} %get-tuple-element.8.hidden_ref, bf16[4,64,128]{2,1,0:T(8,128)(2,1)} %fusion.4.route_ref, bf16[1,3584,1024]{2,1,0:T(8,128)(2,1)} %gate_hbm.1, bf16[1,1024,3584]{2,1,0:T(8,128)(2,1)} %down_hbm.1), custom_call_target="tpu_custom_call" | custom-call | tf_op jit(solution)/shard_map/pallas_call | solution.py:358
  77.7 1.6 %convert_element_type.25 = bf16[16,3584]{1,0:T(8,128)(2,1)} convert(f32[16,3584]{1,0:T(8,128)} %shard_map.128) | non-fusion elementwise | flops 57344 | bytes 344064 | tf_op jit(solution)/shard_map/convert_element_type | solution.py:383
  (10 shorter events, 0.1 us)
Async XLA Ops:
  0.0 29.6 %copy-start = (f32[16,8]{0,1:T(8,128)S(1)}, f32[16,8]{0,1:T(8,128)}, u32[]{:S(2)}) copy-start(f32[16,8]{0,1:T(8,128)} %param.25) | copy-start | bytes 1540
  0.0 29.7 %copy-start.1 = (s32[16,8]{0,1:T(8,128)S(1)}, s32[16,8]{0,1:T(8,128)}, u32[]{:S(2)}) copy-start(s32[16,8]{0,1:T(8,128)} %param.24) | copy-start | bytes 1540
